TPU v7x, 128 devices: a whole 4x4x4 slice. The times are simulated.
128 devices in a mesh: dp: 8 (over x, core), rollout: 16 (over y, z).
Axes of the slice: x: 4, y: 4, z: 4, core: 2. Of those that a mesh axis runs over, the one named last changes fastest.
Arguments:
- queries: bfloat16 [128, 512, 2560], P(('dp', 'rollout')), may hold values from -100 to 100
- resp_keys: bfloat16 [128, 512, 512], P(('dp', 'rollout')), may hold values from -5 to 5
- resp_values: bfloat16 [128, 512, 512], P(('dp', 'rollout')), may hold values from -6 to 6
- prompt_keys: bfloat16 [8, 256, 512], P('dp', 'rollout'), may hold values from -6 to 6
- prompt_values: bfloat16 [8, 256, 512], P('dp', 'rollout'), may hold values from -6 to 6
- d_out: bfloat16 [128, 512, 2560], P(('dp', 'rollout')), may hold values from -6 to 6
- lengths: int32 [128], replicated, may hold values from 64 to 512
- owner: int32 [128], replicated, may hold values from 0 to 7
Outputs:
- attn_out: bfloat16 [128, 512, 2560], P(('dp', 'rollout'))
- d_queries: bfloat16 [128, 512, 2560], P(('dp', 'rollout'))
- d_resp_keys: bfloat16 [128, 512, 512], P(('dp', 'rollout'))
- d_resp_values: bfloat16 [128, 512, 512], P(('dp', 'rollout'))
- d_prompt_keys: float32 [8, 256, 512], P('dp', 'rollout')
- d_prompt_values: float32 [8, 256, 512], P('dp', 'rollout')
Inputs may be any that keep to these rules, and one draw needn't show every extreme that they name: `lengths`: rows of a block at or past its length are padding.
All inputs are finite; a program needn't handle non-finite values.
Results may differ from a plain program's by a relative error of at most 0.0071.
Values may be sent and summed in bfloat16 or wider, within the bound.
No kernel may reach another device: no remote copies, remote signals or barrier semaphores. Data moves between devices by JAX's collectives and lax.ppermute only.
A program may use at most 128 MiB of HBM per device.

v0:
```python
import jax
import jax.numpy as jnp
from jax import lax
from jax.sharding import PartitionSpec as P

HEAD_DIM = 128
BLOCK = 512
TILE = 128


def cut_along(shard, dim, count):
    dims = shard.shape
    pieces = shard.reshape(*dims[:dim], count, dims[dim] // count, *dims[dim + 1 :])
    return jnp.moveaxis(pieces, dim, 0)


def sent_and_summed(shard, axis, dim):
    pieces = cut_along(shard, dim, lax.axis_size(axis))
    arrived = lax.all_to_all(pieces, axis, split_axis=0, concat_axis=0, tiled=True)
    return arrived.astype(jnp.float32).sum(axis=0)


def attend(q_rows, d_rows, offset, stride, length, keys, values):
    rows = q_rows.shape[0]
    span = keys.shape[0]
    kv_heads = keys.shape[1] // HEAD_DIM
    group = q_rows.shape[1] // keys.shape[1]
    key_heads = keys.reshape(span, kv_heads, HEAD_DIM)
    val_heads = values.reshape(span, kv_heads, HEAD_DIM)
    key_pos = jnp.arange(span, dtype=jnp.int32) - (span - BLOCK)
    live_rows = jnp.clip((length - offset + stride - 1) // stride, 0, rows)
    turns = (live_rows + TILE - 1) // TILE
    scale = HEAD_DIM ** (-0.5)

    def step(turn, carry):
        out_all, dq_all, dk_sum, dv_sum = carry
        start = (turn * TILE).astype(jnp.int32)
        qt = lax.dynamic_slice_in_dim(q_rows, start, TILE, 0).reshape(
            TILE, kv_heads, group, HEAD_DIM
        )
        dt = lax.dynamic_slice_in_dim(d_rows, start, TILE, 0)
        pos = offset + stride * (start + jnp.arange(TILE, dtype=jnp.int32))
        live = pos < length
        dt = jnp.where(live[:, None], dt, jnp.zeros_like(dt)).reshape(
            TILE, kv_heads, group, HEAD_DIM
        )
        scores = (
            jnp.einsum("tkgd,skd->kgts", qt, key_heads, preferred_element_type=jnp.float32) * scale
        )
        allowed = key_pos[None, :] <= pos[:, None]
        scores = jnp.where(allowed, scores, -1e30)
        top = jnp.max(scores, axis=-1, keepdims=True)
        expd = jnp.exp(scores - top)
        probs = expd / jnp.sum(expd, axis=-1, keepdims=True)
        weights = probs.astype(jnp.bfloat16)
        out = jnp.einsum("kgts,skd->tkgd", weights, val_heads, preferred_element_type=jnp.float32)
        out = out * live.astype(jnp.float32)[:, None, None, None]
        dprob = jnp.einsum("tkgd,skd->kgts", dt, val_heads, preferred_element_type=jnp.float32)
        delta = jnp.einsum("tkgd,tkgd->kgt", dt.astype(jnp.float32), out)
        dscore = (probs * (dprob - delta[..., None]) * scale).astype(jnp.bfloat16)
        dq = jnp.einsum("kgts,skd->tkgd", dscore, key_heads, preferred_element_type=jnp.float32)
        dk_sum = dk_sum + jnp.einsum(
            "kgts,tkgd->skd", dscore, qt, preferred_element_type=jnp.float32
        )
        dv_sum = dv_sum + jnp.einsum(
            "kgts,tkgd->skd", weights, dt, preferred_element_type=jnp.float32
        )
        out_all = lax.dynamic_update_slice_in_dim(
            out_all, out.reshape(TILE, -1).astype(jnp.bfloat16), start, 0
        )
        dq_all = lax.dynamic_update_slice_in_dim(
            dq_all, dq.reshape(TILE, -1).astype(jnp.bfloat16), start, 0
        )
        return (out_all, dq_all, dk_sum, dv_sum)

    init = (
        jnp.zeros((rows, q_rows.shape[1]), jnp.bfloat16),
        jnp.zeros((rows, q_rows.shape[1]), jnp.bfloat16),
        jnp.zeros((span, kv_heads, HEAD_DIM), jnp.float32),
        jnp.zeros((span, kv_heads, HEAD_DIM), jnp.float32),
    )
    out_all, dq_all, dk_sum, dv_sum = lax.fori_loop(jnp.int32(0), turns, step, init)
    return (out_all, dq_all, dk_sum.reshape(span, -1), dv_sum.reshape(span, -1))


def block_inputs(whole_prompt, group_index, keys_block, values_block, width_k):
    prompt_pair = lax.dynamic_index_in_dim(whole_prompt, group_index, 0, keepdims=False)
    keys = jnp.concatenate([prompt_pair[:, :width_k], keys_block], axis=0)
    values = jnp.concatenate([prompt_pair[:, width_k:], values_block], axis=0)
    return (keys, values)


def per_device(queries, resp_keys, resp_values, prompt_keys, prompt_values, d_out, lengths, owner):
    rollout_count = lax.axis_size("rollout")
    groups = lax.axis_size("dp")
    row_base = lax.axis_index("dp") * rollout_count
    here = row_base + lax.axis_index("rollout")
    shard_rows = prompt_keys.shape[1]
    prompt_n = shard_rows * rollout_count
    width_k = prompt_keys.shape[2]
    local_pair = jnp.concatenate([prompt_keys[0], prompt_values[0]], axis=1)
    gathered = lax.all_gather(local_pair, ("dp", "rollout"), axis=0, tiled=True)
    whole_prompt = gathered.reshape(groups, prompt_n, 2 * width_k)
    group_ids = jnp.arange(groups, dtype=jnp.int32)
    own_group = owner[here]
    own_keys, own_values = block_inputs(
        whole_prompt, own_group, resp_keys[0], resp_values[0], width_k
    )
    row_owner = lax.dynamic_slice_in_dim(owner, row_base, rollout_count, 0)
    out, dq, dk_all, dv_all = attend(
        queries[0], d_out[0], 0, 1, lengths[here], own_keys, own_values
    )
    dk_resp = dk_all[prompt_n:]
    dv_resp = dv_all[prompt_n:]
    terms = jnp.concatenate([dk_all[:prompt_n], dv_all[:prompt_n]], axis=1)[None]
    source_groups = row_owner[None]
    pieces = terms.reshape(terms.shape[0], rollout_count, shard_rows, 2 * width_k)
    received = lax.all_to_all(
        pieces.astype(jnp.bfloat16), "rollout", split_axis=1, concat_axis=1, tiled=True
    ).astype(pieces.dtype)
    picks = (source_groups[:, :, None] == group_ids[None, None, :]).astype(jnp.float32)
    by_group = jnp.einsum("msg,msrc->grc", picks, received, precision=lax.Precision.HIGHEST)
    summed = sent_and_summed(by_group.astype(jnp.bfloat16), "dp", 0)[0]
    return (
        out[None],
        dq[None],
        dk_resp.astype(jnp.bfloat16)[None],
        dv_resp.astype(jnp.bfloat16)[None],
        summed[None, :, :width_k],
        summed[None, :, width_k:],
    )


def solution(mesh):
    placed = (
        P(("dp", "rollout"), None, None),
        P(("dp", "rollout"), None, None),
        P(("dp", "rollout"), None, None),
        P("dp", "rollout", None),
        P("dp", "rollout", None),
        P(("dp", "rollout"), None, None),
        P(),
        P(),
    )
    return jax.shard_map(
        per_device,
        mesh=mesh,
        in_specs=placed,
        out_specs=(
            P(("dp", "rollout"), None, None),
            P(("dp", "rollout"), None, None),
            P(("dp", "rollout"), None, None),
            P(("dp", "rollout"), None, None),
            P("dp", "rollout", None),
            P("dp", "rollout", None),
        ),
        check_vma=False,
    )
```

profile of v0, /device:TPU:1, one launch (start us, length us, event | category | flops | bytes accessed | tf_op | source)
XLA Modules:
  0.0 223.8 jit_solution(10658430492384995604)
XLA Ops:
  7.2 1.4 pad_maximum_fusion.2
  8.6 1.2 dynamic_slice.19
  10.5 1.2 dynamic_slice.20
  13.1 1.3 copy.49
  14.3 2.0 copy.50
  16.4 4.5 %copy.47 = bf16[1,512,2560]{1,2,0:T(8,128)(2,1)} copy(bf16[1,512,2560]{2,1,0:T(8,128)(2,1)} %param.10) | data formatting | bytes 5242880 | tf_op args[0]
  20.9 2.6 %copy.51 = bf16[1,512,2560]{1,2,0:T(8,128)(2,1)} copy(bf16[1,512,2560]{2,1,0:T(8,128)(2,1)S(1)} %copy-done.5) | data formatting | bytes 5242880 | tf_op args[5]
  24.3 57.5 %all-gather.2.cloned.1.call-done = bf16[2048,1024]{1,0:T(8,128)(2,1)} async-done(((bf16[16,1024]{1,0:T(8,128)(2,1)}), bf16[2048,1024]{1,0:T(8,128)(2,1)}) %all-gather.2.cloned.1.call-update) | async-done | bytes 4194320 | tf_op jit(solution)/shard_map/all_gather | solution.py:102
  81.8 1.1 constant_dynamic-slice_fusion.1
  83.2 1.2 copy.52
  85.5 1.3 broadcast.74
  86.8 1.7 broadcast.73.clone2
  88.4 1.7 broadcast.73.clone
  90.1 95.3 %while.17 = (s32[]{:T(128)}, bf16[512,2560]{1,0:T(8,128)(2,1)}, bf16[512,2560]{1,0:T(8,128)(2,1)}, f32[768,4,128]{0,2,1:T(8,128)}, f32[768,4,128]{0,2,1:T(8,128)...) while((s32[]{:T(128)}, bf16[512,2560]{1,0:T(8,128)(2,1)}, ...), condition=%wide.region_3.4_spmd.clone, body=%wide.region_0.3_spmd.clone.sunk | while | flops 3048635904 | bytes 116517448 | solution.py:82
  90.9 1.5 dynamic-slice_select_fusion.2
  92.3 2.4 %fusion.68 = f32[4,128,5,768]{3,1,2,0:T(8,128)S(1)} fusion(bf16[128,4,5,128]{0,3,2,1:T(8,128)(2,1)S(1)} %bitcast.145, bf16[768,4,128]{0,2,1:T(8,128)(2,1)} %get-tuple-element.278), kind=kOutput, calls=%fused_computation.26.clone.1 | convolution fusion | flops 503316480 | bytes 9306112 | tf_op jit(solution)/shard_map/while/body/tkgd,skd->kgts/dot_general | solution.py:48
  94.7 3.7 %fusion.69 = (f32[4,5,128]{2,1,0:T(8,128)S(1)}, f32[4,5,128,768]{3,2,1,0:T(8,128)S(1)}) fusion(f32[4,128,5,768]{3,1,2,0:T(8,128)S(1)} %fusion.68, pred[128,768]{1,0:T(8,128)(4,1)S(1)} %broadcast_compare_fusion.4), kind=kOutput, calls=%fused_computation.54.clone.1 | output fusion | flops 11797247 | bytes 15837184 | tf_op jit(solution)/shard_map/while/body/sub | solution.py:53
  99.5 1.3 fusion.71
  101.8 3.6 %fusion.72 = bf16[4,5,128,768]{3,2,1,0:T(8,128)(2,1)} fusion(f32[4,5,128]{2,1,0:T(8,128)S(1)} %get-tuple-element.240, f32[4,5,128,768]{3,2,1,0:T(8,128)S(1)} %get-tuple-element.237, f32[4,5,128]{2,1,0:T(8,128)S(1)} %get-tuple-element.238, bf16[128,4,5,128]{0,3,2,1:T(8,128)(2,1)S(1)} %bitcast.149, bf16[768,4,128]{2,0,1:T(8,128)(2,1)S(1)} %copy-done.7), kind=kOutput, calls=%fused_computation.5.clone.1 | convolution fusion | flops 513146880 | bytes 13258752 | tf_op jit(solution)/shard_map/while/body/tkgd,skd->kgts/dot_general | solution.py:58
  105.7 3.7 %convolution_convert_fusion.3 = bf16[4,5,128,128]{2,3,1,0:T(8,128)(2,1)S(1)} fusion(bf16[4,5,128,768]{3,2,1,0:T(8,128)(2,1)} %fusion.72, bf16[768,4,128]{0,2,1:T(8,128)(2,1)} %get-tuple-element.278), kind=kOutput, calls=%fused_computation.19.clone.1 | convolution fusion | flops 503644160 | bytes 5373952 | tf_op jit(solution)/shard_map/while/body/kgts,skd->tkgd/dot_general | solution.py:61
  110.7 1.2 copy-done.2
  114.7 1.5 dynamic-slice_select_fusion.2
  116.2 2.4 %fusion.68 = f32[4,128,5,768]{3,1,2,0:T(8,128)S(1)} fusion(bf16[128,4,5,128]{0,3,2,1:T(8,128)(2,1)S(1)} %bitcast.145, bf16[768,4,128]{0,2,1:T(8,128)(2,1)} %get-tuple-element.278), kind=kOutput, calls=%fused_computation.26.clone.1 | convolution fusion | flops 503316480 | bytes 9306112 | tf_op jit(solution)/shard_map/while/body/tkgd,skd->kgts/dot_general | solution.py:48
  118.5 3.7 %fusion.69 = (f32[4,5,128]{2,1,0:T(8,128)S(1)}, f32[4,5,128,768]{3,2,1,0:T(8,128)S(1)}) fusion(f32[4,128,5,768]{3,1,2,0:T(8,128)S(1)} %fusion.68, pred[128,768]{1,0:T(8,128)(4,1)S(1)} %broadcast_compare_fusion.4), kind=kOutput, calls=%fused_computation.54.clone.1 | output fusion | flops 11797247 | bytes 15837184 | tf_op jit(solution)/shard_map/while/body/sub | solution.py:53
  123.4 1.3 fusion.71
  125.7 3.6 %fusion.72 = bf16[4,5,128,768]{3,2,1,0:T(8,128)(2,1)} fusion(f32[4,5,128]{2,1,0:T(8,128)S(1)} %get-tuple-element.240, f32[4,5,128,768]{3,2,1,0:T(8,128)S(1)} %get-tuple-element.237, f32[4,5,128]{2,1,0:T(8,128)S(1)} %get-tuple-element.238, bf16[128,4,5,128]{0,3,2,1:T(8,128)(2,1)S(1)} %bitcast.149, bf16[768,4,128]{2,0,1:T(8,128)(2,1)S(1)} %copy-done.7), kind=kOutput, calls=%fused_computation.5.clone.1 | convolution fusion | flops 513146880 | bytes 13258752 | tf_op jit(solution)/shard_map/while/body/tkgd,skd->kgts/dot_general | solution.py:58
  129.6 3.7 %convolution_convert_fusion.3 = bf16[4,5,128,128]{2,3,1,0:T(8,128)(2,1)S(1)} fusion(bf16[4,5,128,768]{3,2,1,0:T(8,128)(2,1)} %fusion.72, bf16[768,4,128]{0,2,1:T(8,128)(2,1)} %get-tuple-element.278), kind=kOutput, calls=%fused_computation.19.clone.1 | convolution fusion | flops 503644160 | bytes 5373952 | tf_op jit(solution)/shard_map/while/body/kgts,skd->tkgd/dot_general | solution.py:61
  134.6 1.2 copy-done.2
  138.5 1.5 dynamic-slice_select_fusion.2
  140.0 2.4 %fusion.68 = f32[4,128,5,768]{3,1,2,0:T(8,128)S(1)} fusion(bf16[128,4,5,128]{0,3,2,1:T(8,128)(2,1)S(1)} %bitcast.145, bf16[768,4,128]{0,2,1:T(8,128)(2,1)} %get-tuple-element.278), kind=kOutput, calls=%fused_computation.26.clone.1 | convolution fusion | flops 503316480 | bytes 9306112 | tf_op jit(solution)/shard_map/while/body/tkgd,skd->kgts/dot_general | solution.py:48
  142.4 3.7 %fusion.69 = (f32[4,5,128]{2,1,0:T(8,128)S(1)}, f32[4,5,128,768]{3,2,1,0:T(8,128)S(1)}) fusion(f32[4,128,5,768]{3,1,2,0:T(8,128)S(1)} %fusion.68, pred[128,768]{1,0:T(8,128)(4,1)S(1)} %broadcast_compare_fusion.4), kind=kOutput, calls=%fused_computation.54.clone.1 | output fusion | flops 11797247 | bytes 15837184 | tf_op jit(solution)/shard_map/while/body/sub | solution.py:53
  147.2 1.3 fusion.71
  149.5 3.6 %fusion.72 = bf16[4,5,128,768]{3,2,1,0:T(8,128)(2,1)} fusion(f32[4,5,128]{2,1,0:T(8,128)S(1)} %get-tuple-element.240, f32[4,5,128,768]{3,2,1,0:T(8,128)S(1)} %get-tuple-element.237, f32[4,5,128]{2,1,0:T(8,128)S(1)} %get-tuple-element.238, bf16[128,4,5,128]{0,3,2,1:T(8,128)(2,1)S(1)} %bitcast.149, bf16[768,4,128]{2,0,1:T(8,128)(2,1)S(1)} %copy-done.7), kind=kOutput, calls=%fused_computation.5.clone.1 | convolution fusion | flops 513146880 | bytes 13258752 | tf_op jit(solution)/shard_map/while/body/tkgd,skd->kgts/dot_general | solution.py:58
  153.4 3.7 %convolution_convert_fusion.3 = bf16[4,5,128,128]{2,3,1,0:T(8,128)(2,1)S(1)} fusion(bf16[4,5,128,768]{3,2,1,0:T(8,128)(2,1)} %fusion.72, bf16[768,4,128]{0,2,1:T(8,128)(2,1)} %get-tuple-element.278), kind=kOutput, calls=%fused_computation.19.clone.1 | convolution fusion | flops 503644160 | bytes 5373952 | tf_op jit(solution)/shard_map/while/body/kgts,skd->tkgd/dot_general | solution.py:61
  158.4 1.2 copy-done.2
  162.4 1.5 dynamic-slice_select_fusion.2
  163.8 2.4 %fusion.68 = f32[4,128,5,768]{3,1,2,0:T(8,128)S(1)} fusion(bf16[128,4,5,128]{0,3,2,1:T(8,128)(2,1)S(1)} %bitcast.145, bf16[768,4,128]{0,2,1:T(8,128)(2,1)} %get-tuple-element.278), kind=kOutput, calls=%fused_computation.26.clone.1 | convolution fusion | flops 503316480 | bytes 9306112 | tf_op jit(solution)/shard_map/while/body/tkgd,skd->kgts/dot_general | solution.py:48
  166.2 3.7 %fusion.69 = (f32[4,5,128]{2,1,0:T(8,128)S(1)}, f32[4,5,128,768]{3,2,1,0:T(8,128)S(1)}) fusion(f32[4,128,5,768]{3,1,2,0:T(8,128)S(1)} %fusion.68, pred[128,768]{1,0:T(8,128)(4,1)S(1)} %broadcast_compare_fusion.4), kind=kOutput, calls=%fused_computation.54.clone.1 | output fusion | flops 11797247 | bytes 15837184 | tf_op jit(solution)/shard_map/while/body/sub | solution.py:53
  171.0 1.3 fusion.71
  173.3 3.6 %fusion.72 = bf16[4,5,128,768]{3,2,1,0:T(8,128)(2,1)} fusion(f32[4,5,128]{2,1,0:T(8,128)S(1)} %get-tuple-element.240, f32[4,5,128,768]{3,2,1,0:T(8,128)S(1)} %get-tuple-element.237, f32[4,5,128]{2,1,0:T(8,128)S(1)} %get-tuple-element.238, bf16[128,4,5,128]{0,3,2,1:T(8,128)(2,1)S(1)} %bitcast.149, bf16[768,4,128]{2,0,1:T(8,128)(2,1)S(1)} %copy-done.7), kind=kOutput, calls=%fused_computation.5.clone.1 | convolution fusion | flops 513146880 | bytes 13258752 | tf_op jit(solution)/shard_map/while/body/tkgd,skd->kgts/dot_general | solution.py:58
  177.2 3.7 %convolution_convert_fusion.3 = bf16[4,5,128,128]{2,3,1,0:T(8,128)(2,1)S(1)} fusion(bf16[4,5,128,768]{3,2,1,0:T(8,128)(2,1)} %fusion.72, bf16[768,4,128]{0,2,1:T(8,128)(2,1)} %get-tuple-element.278), kind=kOutput, calls=%fused_computation.19.clone.1 | convolution fusion | flops 503644160 | bytes 5373952 | tf_op jit(solution)/shard_map/while/body/kgts,skd->tkgd/dot_general | solution.py:61
  182.2 1.2 copy-done.2
  188.4 4.4 %all-to-all-start = ((bf16[1,16,16,1024]{3,2,0,1:T(8,128)(2,1)}), bf16[1,16,16,1024]{3,2,0,1:T(8,128)(2,1)S(1)}, u32[]{:S(2)}, u32[]{:S(2)}) async-start(bf16[1,16,16,1024]{3,2,0,1:T(8,128)(2,1)} %maximum_bitcast_fusion), calls=%async_computation | async-start | bytes 1048576 | tf_op jit(solution)/shard_map/all_to_all | solution.py:118
  192.8 10.0 %all-to-all-done = bf16[1,16,16,1024]{3,2,0,1:T(8,128)(2,1)S(1)} async-done(((bf16[1,16,16,1024]{3,2,0,1:T(8,128)(2,1)}), bf16[1,16,16,1024]{3,2,0,1:T(8,128)(2,1)S(1)}, u32[]{:S(2)}, u32[]{:S(2)}) %all-to-all-start) | async-done | bytes 524320 | tf_op jit(solution)/shard_map/all_to_all | solution.py:118
  204.1 5.6 %all-to-all-start.1 = ((bf16[8,1,16,1024]{3,2,1,0:T(8,128)(2,1)}), bf16[8,1,16,1024]{3,2,1,0:T(8,128)(2,1)S(1)}, u32[]{:S(2)}, u32[]{:S(2)}) async-start(bf16[8,1,16,1024]{3,2,1,0:T(8,128)(2,1)} %copy.61), calls=%async_computation.1 | async-start | bytes 524288 | tf_op jit(solution)/shard_map/all_to_all | solution.py:19
  209.8 1.0 copy.77
  210.8 1.0 copy.76
  211.8 4.4 %all-to-all-done.1 = bf16[8,1,16,1024]{3,2,1,0:T(8,128)(2,1)S(1)} async-done(((bf16[8,1,16,1024]{3,2,1,0:T(8,128)(2,1)}), bf16[8,1,16,1024]{3,2,1,0:T(8,128)(2,1)S(1)}, u32[]{:S(2)}, u32[]{:S(2)}) %all-to-all-start.1) | async-done | bytes 262176 | tf_op jit(solution)/shard_map/all_to_all | solution.py:19
  (106 shorter events, 31.9 us)
Async XLA Ops:
  7.2 74.6 %all-gather.2.cloned.1.call-start = ((), (), s32[]{:S(2)}) async-start(), calls=%async_computation.2 | async-start | bytes 4227072 | tf_op jit(solution)/shard_map/all_gather | solution.py:102
  16.4 4.6 %copy-start.5 = (bf16[1,512,2560]{2,1,0:T(8,128)(2,1)S(1)}, bf16[1,512,2560]{2,1,0:T(8,128)(2,1)}, u32[]{:S(2)}) copy-start(bf16[1,512,2560]{2,1,0:T(8,128)(2,1)} %param.15) | copy-start | bytes 7864324
  23.5 59.6 %copy-start.6 = (bf16[1,512,512]{1,2,0:T(8,128)(2,1)S(1)}, bf16[1,512,512]{1,2,0:T(8,128)(2,1)}, u32[]{:S(2)}) copy-start(bf16[1,512,512]{1,2,0:T(8,128)(2,1)} %copy.50) | copy-start | bytes 1572868
  98.4 1.1 copy-start.7
  105.7 3.8 %copy-start = (bf16[4,5,128,768]{3,2,1,0:T(8,128)(2,1)S(1)}, bf16[4,5,128,768]{3,2,1,0:T(8,128)(2,1)}, u32[]{:S(2)}) copy-start(bf16[4,5,128,768]{3,2,1,0:T(8,128)(2,1)} %fusion.72) | copy-start | bytes 11796484 | tf_op jit(solution)/shard_map/while
  105.7 4.0 %copy-start.1 = (f32[768,4,128]{0,2,1:T(8,128)S(1)}, f32[768,4,128]{0,2,1:T(8,128)}, u32[]{:S(2)}) copy-start(f32[768,4,128]{0,2,1:T(8,128)} %get-tuple-element.259) | copy-start | bytes 4718596 | tf_op jit(solution)/shard_map/while
  110.7 1.2 copy-start.2
  122.2 1.1 copy-start.7
  129.6 3.8 %copy-start = (bf16[4,5,128,768]{3,2,1,0:T(8,128)(2,1)S(1)}, bf16[4,5,128,768]{3,2,1,0:T(8,128)(2,1)}, u32[]{:S(2)}) copy-start(bf16[4,5,128,768]{3,2,1,0:T(8,128)(2,1)} %fusion.72) | copy-start | bytes 11796484 | tf_op jit(solution)/shard_map/while
  129.6 4.0 %copy-start.1 = (f32[768,4,128]{0,2,1:T(8,128)S(1)}, f32[768,4,128]{0,2,1:T(8,128)}, u32[]{:S(2)}) copy-start(f32[768,4,128]{0,2,1:T(8,128)} %get-tuple-element.259) | copy-start | bytes 4718596 | tf_op jit(solution)/shard_map/while
  134.6 1.2 copy-start.2
  146.1 1.1 copy-start.7
  153.4 3.8 %copy-start = (bf16[4,5,128,768]{3,2,1,0:T(8,128)(2,1)S(1)}, bf16[4,5,128,768]{3,2,1,0:T(8,128)(2,1)}, u32[]{:S(2)}) copy-start(bf16[4,5,128,768]{3,2,1,0:T(8,128)(2,1)} %fusion.72) | copy-start | bytes 11796484 | tf_op jit(solution)/shard_map/while
  153.4 4.0 %copy-start.1 = (f32[768,4,128]{0,2,1:T(8,128)S(1)}, f32[768,4,128]{0,2,1:T(8,128)}, u32[]{:S(2)}) copy-start(f32[768,4,128]{0,2,1:T(8,128)} %get-tuple-element.259) | copy-start | bytes 4718596 | tf_op jit(solution)/shard_map/while
  158.4 1.2 copy-start.2
  169.9 1.1 copy-start.7
  177.2 3.8 %copy-start = (bf16[4,5,128,768]{3,2,1,0:T(8,128)(2,1)S(1)}, bf16[4,5,128,768]{3,2,1,0:T(8,128)(2,1)}, u32[]{:S(2)}) copy-start(bf16[4,5,128,768]{3,2,1,0:T(8,128)(2,1)} %fusion.72) | copy-start | bytes 11796484 | tf_op jit(solution)/shard_map/while
  177.2 4.0 %copy-start.1 = (f32[768,4,128]{0,2,1:T(8,128)S(1)}, f32[768,4,128]{0,2,1:T(8,128)}, u32[]{:S(2)}) copy-start(f32[768,4,128]{0,2,1:T(8,128)} %get-tuple-element.259) | copy-start | bytes 4718596 | tf_op jit(solution)/shard_map/while
  182.2 1.2 copy-start.2
  185.4 1.7 copy-start.3
  185.5 0.9 copy-start.4
  187.1 5.6 %copy-start.8 = (s32[128]{0:T(128)S(1)}, s32[128]{0:T(128)}, u32[]{:S(2)}) copy-start(s32[128]{0:T(128)} %param.17) | copy-start | bytes 1540
  188.4 21.4 %slice-start = ((bf16[768,4,128]{0,2,1:T(8,128)(2,1)}), bf16[512,4,128]{0,2,1:T(8,128)(2,1)S(1)}, s32[]{:S(2)}) async-start(bf16[768,4,128]{0,2,1:T(8,128)(2,1)} %copy-done.4), calls=%async_computation.3 | async-start | bytes 1048576 | tf_op jit(solution)/shard_map/slice | solution.py:114
  188.4 14.5 %all-to-all-start = ((bf16[1,16,16,1024]{3,2,0,1:T(8,128)(2,1)}), bf16[1,16,16,1024]{3,2,0,1:T(8,128)(2,1)S(1)}, u32[]{:S(2)}, u32[]{:S(2)}) async-start(bf16[1,16,16,1024]{3,2,0,1:T(8,128)(2,1)} %maximum_bitcast_fusion), calls=%async_computation | async-start | bytes 1048576 | tf_op jit(solution)/shard_map/all_to_all | solution.py:118
  204.1 12.1 %all-to-all-start.1 = ((bf16[8,1,16,1024]{3,2,1,0:T(8,128)(2,1)}), bf16[8,1,16,1024]{3,2,1,0:T(8,128)(2,1)S(1)}, u32[]{:S(2)}, u32[]{:S(2)}) async-start(bf16[8,1,16,1024]{3,2,1,0:T(8,128)(2,1)} %copy.61), calls=%async_computation.1 | async-start | bytes 524288 | tf_op jit(solution)/shard_map/all_to_all | solution.py:19
Sparse Core Ops, SparseCore 0:
  11.7 70.0 all-gather.1
where the time goes:
time: 225 us; the launch traced here: 224 us
  waiting for transfers between devices  72 us (32%)
  matrix products  52.5 us (23%)
  local copies, waits for them, and re-layouts  42.1 us (19%)
  other arithmetic  29.7 us (13%)
  between operations  16.9 us (8%)
  starting transfers between devices  10 us (4%)
    all_gather x1, waiting for transfers between devices, per_device(): gathered = lax.all_gather(local_pair, ('dp', 'rollout'), axis=0, tiled=True)  57.5 us
    dot_general x4, matrix products, step(): jnp.einsum('kgts,skd->tkgd', dscore, key_heads, preferred_element_type=jn...  14.9 us
    sub x4, other arithmetic, step(): expd = jnp.exp(scores - top)  14.7 us
    dot_general x4, matrix products, step(): jnp.einsum('tkgd,skd->kgts', dt, val_heads, preferred_element_type=jnp.fl...  14.5 us
    unnamed x16, local copies, waits for them, and re-layouts  13.2 us
    all_to_all x1, waiting for transfers between devices, per_device(): lax.all_to_all(pieces.astype(jnp.bfloat16), 'rollout', split_axis=1, conc...  10 us
    dot_general x4, matrix products, step(): jnp.einsum('tkgd,skd->kgts', qt, key_heads, preferred_element_type=jnp.fl...  9.42 us
    while x32, local copies, waits for them, and re-layouts  7.41 us
  transfers between devices with their start and end apart: 3, of which 3 were waited for; matrix products, arithmetic and copies ran while one was open for 7% of the time, Pallas kernels for 0%

commit v1 on v0

--- a/solution.py
+++ b/solution.py
@@ -6,6 +6,13 @@
 HEAD_DIM = 128
 BLOCK = 512
 TILE = 128
+
+
+def swap_blocks(block, axis, split, join):
+    size = lax.axis_size(axis)
+    pieces = jnp.stack(jnp.split(block, size, axis=split), axis=0)
+    pieces = lax.all_to_all(pieces, axis, split_axis=0, concat_axis=0)
+    return jnp.concatenate(pieces, axis=join)
 
 
 def cut_along(shard, dim, count):
@@ -115,9 +122,7 @@
     terms = jnp.concatenate([dk_all[:prompt_n], dv_all[:prompt_n]], axis=1)[None]
     source_groups = row_owner[None]
     pieces = terms.reshape(terms.shape[0], rollout_count, shard_rows, 2 * width_k)
-    received = lax.all_to_all(
-        pieces.astype(jnp.bfloat16), "rollout", split_axis=1, concat_axis=1, tiled=True
-    ).astype(pieces.dtype)
+    received = swap_blocks(pieces.astype(jnp.bfloat16), "rollout", 1, 1).astype(pieces.dtype)
     picks = (source_groups[:, :, None] == group_ids[None, None, :]).astype(jnp.float32)
     by_group = jnp.einsum("msg,msrc->grc", picks, received, precision=lax.Precision.HIGHEST)
     summed = sent_and_summed(by_group.astype(jnp.bfloat16), "dp", 0)[0]

time: 225 us -> 234 us (1.040)
  local copies, waits for them, and re-layouts: 42.1 us -> 52.1 us
    unnamed x16 -> x32, local copies, waits for them, and re-layouts: 13.2 us -> 22.5 us
    another operation x4 -> x5, local copies, waits for them, and re-layouts: 4.74 us -> 5.35 us
  transfers between devices with their start and end apart: 3 -> 3, of which waited for: 3 -> 3; matrix products, arithmetic and copies ran while one was open for 7% -> 6% of each run, Pallas kernels for 0% -> 0%
where the time goes in v1:
time: 234 us; the launch traced here: 233 us
  waiting for transfers between devices  72 us (31%)
  matrix products  52.5 us (22%)
  local copies, waits for them, and re-layouts  52.1 us (22%)
  other arithmetic  28.9 us (12%)
  between operations  16.9 us (7%)
  starting transfers between devices  9.88 us (4%)
    all_gather x1, waiting for transfers between devices, per_device(): gathered = lax.all_gather(local_pair, ('dp', 'rollout'), axis=0, tiled=True)  57.5 us
    unnamed x32, local copies, waits for them, and re-layouts  22.5 us
    dot_general x4, matrix products, step(): jnp.einsum('kgts,skd->tkgd', dscore, key_heads, preferred_element_type=jn...  14.9 us
    sub x4, other arithmetic, step(): expd = jnp.exp(scores - top)  14.7 us
    dot_general x4, matrix products, step(): jnp.einsum('tkgd,skd->kgts', dt, val_heads, preferred_element_type=jnp.fl...  14.5 us
    all_to_all x1, waiting for transfers between devices, swap_blocks(): pieces = lax.all_to_all(pieces, axis, split_axis=0, concat_axis=0)  10 us
    dot_general x4, matrix products, step(): jnp.einsum('tkgd,skd->kgts', qt, key_heads, preferred_element_type=jnp.fl...  9.42 us
    while x32, local copies, waits for them, and re-layouts  7.41 us
  transfers between devices with their start and end apart: 3, of which 3 were waited for; matrix products, arithmetic and copies ran while one was open for 6% of the time, Pallas kernels for 0%

profile of v1, /device:TPU:1, one launch (start us, length us, event | category | flops | bytes accessed | tf_op | source)
XLA Modules:
  0.0 232.7 jit_solution(5848726425246212452)
XLA Ops:
  7.2 1.4 pad_maximum_fusion.2
  8.6 1.2 dynamic_slice.19
  10.5 1.2 dynamic_slice.20
  13.1 1.3 copy.545
  14.3 2.0 copy.546
  16.4 4.5 %copy.543 = bf16[1,512,2560]{1,2,0:T(8,128)(2,1)} copy(bf16[1,512,2560]{2,1,0:T(8,128)(2,1)} %param.10) | data formatting | bytes 5242880 | tf_op args[0]
  20.9 2.6 %copy.547 = bf16[1,512,2560]{1,2,0:T(8,128)(2,1)} copy(bf16[1,512,2560]{2,1,0:T(8,128)(2,1)S(1)} %copy-done.5) | data formatting | bytes 5242880 | tf_op args[5]
  24.3 57.5 %all-gather.2.cloned.1.call-done = bf16[2048,1024]{1,0:T(8,128)(2,1)} async-done(((bf16[16,1024]{1,0:T(8,128)(2,1)}), bf16[2048,1024]{1,0:T(8,128)(2,1)}) %all-gather.2.cloned.1.call-update) | async-done | bytes 4194320 | tf_op jit(solution)/shard_map/all_gather | solution.py:109
  81.8 1.1 constant_dynamic-slice_fusion.1
  83.2 1.2 copy.548
  85.5 1.3 broadcast.74
  86.8 1.7 broadcast.73.clone2
  88.4 1.7 broadcast.73.clone
  90.1 95.3 %while.17 = (s32[]{:T(128)}, bf16[512,2560]{1,0:T(8,128)(2,1)}, bf16[512,2560]{1,0:T(8,128)(2,1)}, f32[768,4,128]{0,2,1:T(8,128)}, f32[768,4,128]{0,2,1:T(8,128)...) while((s32[]{:T(128)}, bf16[512,2560]{1,0:T(8,128)(2,1)}, ...), condition=%wide.region_3.4_spmd.clone, body=%wide.region_0.3_spmd.clone.sunk | while | flops 3048635904 | bytes 116517448 | solution.py:89
  90.9 1.5 dynamic-slice_select_fusion.2
  92.3 2.4 %fusion.68 = f32[4,128,5,768]{3,1,2,0:T(8,128)S(1)} fusion(bf16[128,4,5,128]{0,3,2,1:T(8,128)(2,1)S(1)} %bitcast.207, bf16[768,4,128]{0,2,1:T(8,128)(2,1)} %get-tuple-element.443), kind=kOutput, calls=%fused_computation.26.clone.1 | convolution fusion | flops 503316480 | bytes 9306112 | tf_op jit(solution)/shard_map/while/body/tkgd,skd->kgts/dot_general | solution.py:55
  94.7 3.7 %fusion.69 = (f32[4,5,128]{2,1,0:T(8,128)S(1)}, f32[4,5,128,768]{3,2,1,0:T(8,128)S(1)}) fusion(f32[4,128,5,768]{3,1,2,0:T(8,128)S(1)} %fusion.68, pred[128,768]{1,0:T(8,128)(4,1)S(1)} %broadcast_compare_fusion.4), kind=kOutput, calls=%fused_computation.87.clone.1 | output fusion | flops 11797247 | bytes 15837184 | tf_op jit(solution)/shard_map/while/body/sub | solution.py:60
  99.5 1.3 fusion.71
  101.8 3.6 %fusion.72 = bf16[4,5,128,768]{3,2,1,0:T(8,128)(2,1)} fusion(f32[4,5,128]{2,1,0:T(8,128)S(1)} %get-tuple-element.405, f32[4,5,128,768]{3,2,1,0:T(8,128)S(1)} %get-tuple-element.402, f32[4,5,128]{2,1,0:T(8,128)S(1)} %get-tuple-element.403, bf16[128,4,5,128]{0,3,2,1:T(8,128)(2,1)S(1)} %bitcast.211, bf16[768,4,128]{2,0,1:T(8,128)(2,1)S(1)} %copy-done.7), kind=kOutput, calls=%fused_computation.5.clone.1 | convolution fusion | flops 513146880 | bytes 13258752 | tf_op jit(solution)/shard_map/while/body/tkgd,skd->kgts/dot_general | solution.py:65
  105.7 3.7 %convolution_convert_fusion.3 = bf16[4,5,128,128]{2,3,1,0:T(8,128)(2,1)S(1)} fusion(bf16[4,5,128,768]{3,2,1,0:T(8,128)(2,1)} %fusion.72, bf16[768,4,128]{0,2,1:T(8,128)(2,1)} %get-tuple-element.443), kind=kOutput, calls=%fused_computation.19.clone.1 | convolution fusion | flops 503644160 | bytes 5373952 | tf_op jit(solution)/shard_map/while/body/kgts,skd->tkgd/dot_general | solution.py:68
  110.7 1.2 copy-done.2
  114.7 1.5 dynamic-slice_select_fusion.2
  116.2 2.4 %fusion.68 = f32[4,128,5,768]{3,1,2,0:T(8,128)S(1)} fusion(bf16[128,4,5,128]{0,3,2,1:T(8,128)(2,1)S(1)} %bitcast.207, bf16[768,4,128]{0,2,1:T(8,128)(2,1)} %get-tuple-element.443), kind=kOutput, calls=%fused_computation.26.clone.1 | convolution fusion | flops 503316480 | bytes 9306112 | tf_op jit(solution)/shard_map/while/body/tkgd,skd->kgts/dot_general | solution.py:55
  118.5 3.7 %fusion.69 = (f32[4,5,128]{2,1,0:T(8,128)S(1)}, f32[4,5,128,768]{3,2,1,0:T(8,128)S(1)}) fusion(f32[4,128,5,768]{3,1,2,0:T(8,128)S(1)} %fusion.68, pred[128,768]{1,0:T(8,128)(4,1)S(1)} %broadcast_compare_fusion.4), kind=kOutput, calls=%fused_computation.87.clone.1 | output fusion | flops 11797247 | bytes 15837184 | tf_op jit(solution)/shard_map/while/body/sub | solution.py:60
  123.4 1.3 fusion.71
  125.7 3.6 %fusion.72 = bf16[4,5,128,768]{3,2,1,0:T(8,128)(2,1)} fusion(f32[4,5,128]{2,1,0:T(8,128)S(1)} %get-tuple-element.405, f32[4,5,128,768]{3,2,1,0:T(8,128)S(1)} %get-tuple-element.402, f32[4,5,128]{2,1,0:T(8,128)S(1)} %get-tuple-element.403, bf16[128,4,5,128]{0,3,2,1:T(8,128)(2,1)S(1)} %bitcast.211, bf16[768,4,128]{2,0,1:T(8,128)(2,1)S(1)} %copy-done.7), kind=kOutput, calls=%fused_computation.5.clone.1 | convolution fusion | flops 513146880 | bytes 13258752 | tf_op jit(solution)/shard_map/while/body/tkgd,skd->kgts/dot_general | solution.py:65
  129.6 3.7 %convolution_convert_fusion.3 = bf16[4,5,128,128]{2,3,1,0:T(8,128)(2,1)S(1)} fusion(bf16[4,5,128,768]{3,2,1,0:T(8,128)(2,1)} %fusion.72, bf16[768,4,128]{0,2,1:T(8,128)(2,1)} %get-tuple-element.443), kind=kOutput, calls=%fused_computation.19.clone.1 | convolution fusion | flops 503644160 | bytes 5373952 | tf_op jit(solution)/shard_map/while/body/kgts,skd->tkgd/dot_general | solution.py:68
  134.6 1.2 copy-done.2
  138.5 1.5 dynamic-slice_select_fusion.2
  140.0 2.4 %fusion.68 = f32[4,128,5,768]{3,1,2,0:T(8,128)S(1)} fusion(bf16[128,4,5,128]{0,3,2,1:T(8,128)(2,1)S(1)} %bitcast.207, bf16[768,4,128]{0,2,1:T(8,128)(2,1)} %get-tuple-element.443), kind=kOutput, calls=%fused_computation.26.clone.1 | convolution fusion | flops 503316480 | bytes 9306112 | tf_op jit(solution)/shard_map/while/body/tkgd,skd->kgts/dot_general | solution.py:55
  142.4 3.7 %fusion.69 = (f32[4,5,128]{2,1,0:T(8,128)S(1)}, f32[4,5,128,768]{3,2,1,0:T(8,128)S(1)}) fusion(f32[4,128,5,768]{3,1,2,0:T(8,128)S(1)} %fusion.68, pred[128,768]{1,0:T(8,128)(4,1)S(1)} %broadcast_compare_fusion.4), kind=kOutput, calls=%fused_computation.87.clone.1 | output fusion | flops 11797247 | bytes 15837184 | tf_op jit(solution)/shard_map/while/body/sub | solution.py:60
  147.2 1.3 fusion.71
  149.5 3.6 %fusion.72 = bf16[4,5,128,768]{3,2,1,0:T(8,128)(2,1)} fusion(f32[4,5,128]{2,1,0:T(8,128)S(1)} %get-tuple-element.405, f32[4,5,128,768]{3,2,1,0:T(8,128)S(1)} %get-tuple-element.402, f32[4,5,128]{2,1,0:T(8,128)S(1)} %get-tuple-element.403, bf16[128,4,5,128]{0,3,2,1:T(8,128)(2,1)S(1)} %bitcast.211, bf16[768,4,128]{2,0,1:T(8,128)(2,1)S(1)} %copy-done.7), kind=kOutput, calls=%fused_computation.5.clone.1 | convolution fusion | flops 513146880 | bytes 13258752 | tf_op jit(solution)/shard_map/while/body/tkgd,skd->kgts/dot_general | solution.py:65
  153.4 3.7 %convolution_convert_fusion.3 = bf16[4,5,128,128]{2,3,1,0:T(8,128)(2,1)S(1)} fusion(bf16[4,5,128,768]{3,2,1,0:T(8,128)(2,1)} %fusion.72, bf16[768,4,128]{0,2,1:T(8,128)(2,1)} %get-tuple-element.443), kind=kOutput, calls=%fused_computation.19.clone.1 | convolution fusion | flops 503644160 | bytes 5373952 | tf_op jit(solution)/shard_map/while/body/kgts,skd->tkgd/dot_general | solution.py:68
  158.4 1.2 copy-done.2
  162.4 1.5 dynamic-slice_select_fusion.2
  163.8 2.4 %fusion.68 = f32[4,128,5,768]{3,1,2,0:T(8,128)S(1)} fusion(bf16[128,4,5,128]{0,3,2,1:T(8,128)(2,1)S(1)} %bitcast.207, bf16[768,4,128]{0,2,1:T(8,128)(2,1)} %get-tuple-element.443), kind=kOutput, calls=%fused_computation.26.clone.1 | convolution fusion | flops 503316480 | bytes 9306112 | tf_op jit(solution)/shard_map/while/body/tkgd,skd->kgts/dot_general | solution.py:55
  166.2 3.7 %fusion.69 = (f32[4,5,128]{2,1,0:T(8,128)S(1)}, f32[4,5,128,768]{3,2,1,0:T(8,128)S(1)}) fusion(f32[4,128,5,768]{3,1,2,0:T(8,128)S(1)} %fusion.68, pred[128,768]{1,0:T(8,128)(4,1)S(1)} %broadcast_compare_fusion.4), kind=kOutput, calls=%fused_computation.87.clone.1 | output fusion | flops 11797247 | bytes 15837184 | tf_op jit(solution)/shard_map/while/body/sub | solution.py:60
  171.0 1.3 fusion.71
  173.3 3.6 %fusion.72 = bf16[4,5,128,768]{3,2,1,0:T(8,128)(2,1)} fusion(f32[4,5,128]{2,1,0:T(8,128)S(1)} %get-tuple-element.405, f32[4,5,128,768]{3,2,1,0:T(8,128)S(1)} %get-tuple-element.402, f32[4,5,128]{2,1,0:T(8,128)S(1)} %get-tuple-element.403, bf16[128,4,5,128]{0,3,2,1:T(8,128)(2,1)S(1)} %bitcast.211, bf16[768,4,128]{2,0,1:T(8,128)(2,1)S(1)} %copy-done.7), kind=kOutput, calls=%fused_computation.5.clone.1 | convolution fusion | flops 513146880 | bytes 13258752 | tf_op jit(solution)/shard_map/while/body/tkgd,skd->kgts/dot_general | solution.py:65
  177.2 3.7 %convolution_convert_fusion.3 = bf16[4,5,128,128]{2,3,1,0:T(8,128)(2,1)S(1)} fusion(bf16[4,5,128,768]{3,2,1,0:T(8,128)(2,1)} %fusion.72, bf16[768,4,128]{0,2,1:T(8,128)(2,1)} %get-tuple-element.443), kind=kOutput, calls=%fused_computation.19.clone.1 | convolution fusion | flops 503644160 | bytes 5373952 | tf_op jit(solution)/shard_map/while/body/kgts,skd->tkgd/dot_general | solution.py:68
  182.2 1.2 copy-done.2
  197.5 4.2 %all-to-all-start = ((bf16[16,1,1,16,1024]{4,3,2,1,0:T(8,128)(2,1)}), bf16[16,1,1,16,1024]{4,3,2,1,0:T(8,128)(2,1)S(1)}, u32[]{:S(2)}, u32[]{:S(2)}) async-start(bf16[16,1,1,16,1024]{4,3,2,1,0:T(8,128)(2,1)} %constant_dynamic-update-slice_fusion.4), calls=%async_computation | async-start | bytes 1048576 | tf_op jit(solution)/shard_map/all_to_all | solution.py:14
  201.8 10.0 %all-to-all-done = bf16[16,1,1,16,1024]{4,3,2,1,0:T(8,128)(2,1)S(1)} async-done(((bf16[16,1,1,16,1024]{4,3,2,1,0:T(8,128)(2,1)}), bf16[16,1,1,16,1024]{4,3,2,1,0:T(8,128)(2,1)S(1)}, u32[]{:S(2)}, u32[]{:S(2)}) %all-to-all-start) | async-done | bytes 524320 | tf_op jit(solution)/shard_map/all_to_all | solution.py:14
  213.1 5.6 %all-to-all-start.1 = ((bf16[8,1,16,1024]{3,2,1,0:T(8,128)(2,1)}), bf16[8,1,16,1024]{3,2,1,0:T(8,128)(2,1)S(1)}, u32[]{:S(2)}, u32[]{:S(2)}) async-start(bf16[8,1,16,1024]{3,2,1,0:T(8,128)(2,1)} %copy.556), calls=%async_computation.1 | async-start | bytes 524288 | tf_op jit(solution)/shard_map/all_to_all | solution.py:26
  218.8 1.0 copy.572
  219.8 1.0 copy.571
  220.8 4.4 %all-to-all-done.1 = bf16[8,1,16,1024]{3,2,1,0:T(8,128)(2,1)S(1)} async-done(((bf16[8,1,16,1024]{3,2,1,0:T(8,128)(2,1)}), bf16[8,1,16,1024]{3,2,1,0:T(8,128)(2,1)S(1)}, u32[]{:S(2)}, u32[]{:S(2)}) %all-to-all-start.1) | async-done | bytes 262176 | tf_op jit(solution)/shard_map/all_to_all | solution.py:26
  (123 shorter events, 41.0 us)
Async XLA Ops:
  7.2 74.6 %all-gather.2.cloned.1.call-start = ((), (), s32[]{:S(2)}) async-start(), calls=%async_computation.2 | async-start | bytes 4227072 | tf_op jit(solution)/shard_map/all_gather | solution.py:109
  16.4 4.6 %copy-start.5 = (bf16[1,512,2560]{2,1,0:T(8,128)(2,1)S(1)}, bf16[1,512,2560]{2,1,0:T(8,128)(2,1)}, u32[]{:S(2)}) copy-start(bf16[1,512,2560]{2,1,0:T(8,128)(2,1)} %param.15) | copy-start | bytes 7864324
  23.5 59.6 %copy-start.6 = (bf16[1,512,512]{1,2,0:T(8,128)(2,1)S(1)}, bf16[1,512,512]{1,2,0:T(8,128)(2,1)}, u32[]{:S(2)}) copy-start(bf16[1,512,512]{1,2,0:T(8,128)(2,1)} %copy.546) | copy-start | bytes 1572868
  98.4 1.1 copy-start.7
  105.7 3.8 %copy-start = (bf16[4,5,128,768]{3,2,1,0:T(8,128)(2,1)S(1)}, bf16[4,5,128,768]{3,2,1,0:T(8,128)(2,1)}, u32[]{:S(2)}) copy-start(bf16[4,5,128,768]{3,2,1,0:T(8,128)(2,1)} %fusion.72) | copy-start | bytes 11796484 | tf_op jit(solution)/shard_map/while
  105.7 4.0 %copy-start.1 = (f32[768,4,128]{0,2,1:T(8,128)S(1)}, f32[768,4,128]{0,2,1:T(8,128)}, u32[]{:S(2)}) copy-start(f32[768,4,128]{0,2,1:T(8,128)} %get-tuple-element.424) | copy-start | bytes 4718596 | tf_op jit(solution)/shard_map/while
  110.7 1.2 copy-start.2
  122.2 1.1 copy-start.7
  129.6 3.8 %copy-start = (bf16[4,5,128,768]{3,2,1,0:T(8,128)(2,1)S(1)}, bf16[4,5,128,768]{3,2,1,0:T(8,128)(2,1)}, u32[]{:S(2)}) copy-start(bf16[4,5,128,768]{3,2,1,0:T(8,128)(2,1)} %fusion.72) | copy-start | bytes 11796484 | tf_op jit(solution)/shard_map/while
  129.6 4.0 %copy-start.1 = (f32[768,4,128]{0,2,1:T(8,128)S(1)}, f32[768,4,128]{0,2,1:T(8,128)}, u32[]{:S(2)}) copy-start(f32[768,4,128]{0,2,1:T(8,128)} %get-tuple-element.424) | copy-start | bytes 4718596 | tf_op jit(solution)/shard_map/while
  134.6 1.2 copy-start.2
  146.1 1.1 copy-start.7
  153.4 3.8 %copy-start = (bf16[4,5,128,768]{3,2,1,0:T(8,128)(2,1)S(1)}, bf16[4,5,128,768]{3,2,1,0:T(8,128)(2,1)}, u32[]{:S(2)}) copy-start(bf16[4,5,128,768]{3,2,1,0:T(8,128)(2,1)} %fusion.72) | copy-start | bytes 11796484 | tf_op jit(solution)/shard_map/while
  153.4 4.0 %copy-start.1 = (f32[768,4,128]{0,2,1:T(8,128)S(1)}, f32[768,4,128]{0,2,1:T(8,128)}, u32[]{:S(2)}) copy-start(f32[768,4,128]{0,2,1:T(8,128)} %get-tuple-element.424) | copy-start | bytes 4718596 | tf_op jit(solution)/shard_map/while
  158.4 1.2 copy-start.2
  169.9 1.1 copy-start.7
  177.2 3.8 %copy-start = (bf16[4,5,128,768]{3,2,1,0:T(8,128)(2,1)S(1)}, bf16[4,5,128,768]{3,2,1,0:T(8,128)(2,1)}, u32[]{:S(2)}) copy-start(bf16[4,5,128,768]{3,2,1,0:T(8,128)(2,1)} %fusion.72) | copy-start | bytes 11796484 | tf_op jit(solution)/shard_map/while
  177.2 4.0 %copy-start.1 = (f32[768,4,128]{0,2,1:T(8,128)S(1)}, f32[768,4,128]{0,2,1:T(8,128)}, u32[]{:S(2)}) copy-start(f32[768,4,128]{0,2,1:T(8,128)} %get-tuple-element.424) | copy-start | bytes 4718596 | tf_op jit(solution)/shard_map/while
  182.2 1.2 copy-start.2
  185.4 1.7 copy-start.3
  185.5 0.9 copy-start.4
  187.2 14.5 %copy-start.8 = (s32[128]{0:T(128)S(1)}, s32[128]{0:T(128)}, u32[]{:S(2)}) copy-start(s32[128]{0:T(128)} %param.17) | copy-start | bytes 1540
  195.0 23.7 %slice-start = ((bf16[768,4,128]{0,2,1:T(8,128)(2,1)}), bf16[512,4,128]{0,2,1:T(8,128)(2,1)S(1)}, s32[]{:S(2)}) async-start(bf16[768,4,128]{0,2,1:T(8,128)(2,1)} %copy-done.4), calls=%async_computation.3 | async-start | bytes 1048576 | tf_op jit(solution)/shard_map/slice | solution.py:121
  197.5 14.4 %all-to-all-start = ((bf16[16,1,1,16,1024]{4,3,2,1,0:T(8,128)(2,1)}), bf16[16,1,1,16,1024]{4,3,2,1,0:T(8,128)(2,1)S(1)}, u32[]{:S(2)}, u32[]{:S(2)}) async-start(bf16[16,1,1,16,1024]{4,3,2,1,0:T(8,128)(2,1)} %constant_dynamic-update-slice_fusion.4), calls=%async_computation | async-start | bytes 1048576 | tf_op jit(solution)/shard_map/all_to_all | solution.py:14
  213.1 12.1 %all-to-all-start.1 = ((bf16[8,1,16,1024]{3,2,1,0:T(8,128)(2,1)}), bf16[8,1,16,1024]{3,2,1,0:T(8,128)(2,1)S(1)}, u32[]{:S(2)}, u32[]{:S(2)}) async-start(bf16[8,1,16,1024]{3,2,1,0:T(8,128)(2,1)} %copy.556), calls=%async_computation.1 | async-start | bytes 524288 | tf_op jit(solution)/shard_map/all_to_all | solution.py:26
Sparse Core Ops, SparseCore 0:
  11.7 70.0 all-gather.1
